TPU v7x, 32 devices: a whole 2x2x4 slice. The times are simulated.
32 devices in a mesh: grp: 2 (over y), wide: 8 (over z, x), narrow: 2 (over core).
Axes of the slice: x: 2, y: 2, z: 4, core: 2. Of those that a mesh axis runs over, the one named last changes fastest.
Arguments:
- cache: bfloat16 [16, 48, 576], P('grp', ('wide', 'narrow')), parts along dimension 0, may hold values from -4 to 4
- lengths: int32 [16], P('grp'), parts along dimension 0, may hold values from 1 to 47, 128 in all
- slots: int32 [16], P('grp'), parts along dimension 0, may hold values from 0 to 7, each once
- query: bfloat16 [16, 1, 64, 576], P(('grp', 'wide'), None, 'narrow'), parts along dimension 0, may hold values from -200 to 200
Outputs:
- attended: bfloat16 [16, 1, 64, 512], P(('grp', 'wide'), None, 'narrow'), parts along dimension 0
There are 2 independent parts, one for each index of `grp`. A program takes and returns all parts, laid end to end along the dimension named above; each array names one. Nothing has to cross between parts.
Inputs may be any that keep to these rules, and one draw needn't show every extreme that they name: `lengths`: each request has at most 47 cached positions, and some request has exactly that many in every draw; its 1 new tokens' entries follow its cached positions. `slots`: A permutation: every slot holds one request.
All inputs are finite; a program needn't handle non-finite values.
Results may differ from a plain program's by a relative error of at most 0.013.
Values may be sent and summed in bfloat16 or wider, within the bound.
A program may use at most 64 MiB of HBM per device.

v0:
```python
import functools

import jax
import jax.numpy as jnp
from jax import lax
from jax.experimental import pallas as pl
from jax.experimental.pallas import tpu as pltpu
from jax.sharding import PartitionSpec as P

LATENT_WIDTH = 512
UNROLL_LIMIT = 16

score_scale = 0.0721687836
floor_value = -1e30


def loop(count, body):
    if count <= UNROLL_LIMIT:
        for step in range(count):
            body(step)
    else:
        lax.fori_loop(0, count, lambda step, carry: (body(step), carry)[1], 0)


def kernel(
    wide_count,
    narrow_count,
    cache_hbm,
    lengths_hbm,
    slots_hbm,
    query_hbm,
    out_ref,
    cache_ref,
    lengths_ref,
    slots_ref,
    query_ref,
    outgoing,
    received,
    local_sem,
    send_sem,
    recv_sem,
):
    wide_index = lax.axis_index("wide")
    narrow_index = lax.axis_index("narrow")
    me = wide_index * narrow_count + narrow_index
    peer_count = wide_count * narrow_count
    shard_rows, request_count, channels = cache_ref.shape
    slab_rows = outgoing.shape[1]

    slots_copy = pltpu.make_async_copy(slots_hbm, slots_ref, local_sem.at[0])
    cache_copy = pltpu.make_async_copy(cache_hbm, cache_ref, local_sem.at[1])
    lengths_copy = pltpu.make_async_copy(lengths_hbm, lengths_ref, local_sem.at[2])
    query_copy = pltpu.make_async_copy(query_hbm, query_ref, local_sem.at[3])
    slots_copy.start()
    cache_copy.start()
    lengths_copy.start()
    query_copy.start()

    def peer(step):
        target = step + (step >= me).astype(jnp.int32)
        return lax.div(target, narrow_count), lax.rem(target, narrow_count)

    barrier = pltpu.get_barrier_semaphore()

    def greet(step):
        wide_peer, narrow_peer = peer(step)
        pl.semaphore_signal(
            barrier,
            inc=1,
            device_id={"wide": wide_peer, "narrow": narrow_peer},
            device_id_type=pl.DeviceIdType.MESH,
        )

    loop(peer_count - 1, greet)
    slots_copy.wait()
    cache_copy.wait()

    slot_row = slots_ref[...].reshape(1, request_count)
    shape = (request_count * slab_rows, request_count)
    row = lax.broadcasted_iota(jnp.int32, shape, 0)
    ordered = None
    for offset in range(shard_rows):
        pick = (slot_row * slab_rows + offset == row).astype(jnp.float32).astype(jnp.bfloat16)
        term = jnp.dot(pick, cache_ref[offset], preferred_element_type=jnp.float32)
        ordered = term if ordered is None else ordered + term
    outgoing[...] = ordered.reshape(outgoing.shape).astype(jnp.bfloat16)
    received[me] = outgoing[wide_index]
    pl.semaphore_wait(barrier, peer_count - 1)

    def send(step):
        wide_peer, narrow_peer = peer(step)
        pltpu.make_async_remote_copy(
            src_ref=outgoing.at[wide_peer],
            dst_ref=received.at[me],
            send_sem=send_sem,
            recv_sem=recv_sem,
            device_id={"wide": wide_peer, "narrow": narrow_peer},
            device_id_type=pl.DeviceIdType.MESH,
        ).start()

    loop(peer_count - 1, send)
    lengths_copy.wait()
    query_copy.wait()
    own_length = jnp.sum(
        jnp.where(
            slot_row == wide_index,
            lengths_ref[...].reshape(1, request_count).astype(jnp.float32),
            0.0,
        ),
        axis=1,
        keepdims=True,
    )
    _, forward_steps, head_count, _ = query_ref.shape
    score_shape = (forward_steps * head_count, peer_count * slab_rows)
    query_rows = query_ref[...].reshape(score_shape[0], channels)
    column = lax.broadcasted_iota(jnp.int32, score_shape, 1)
    offset = column % slab_rows
    place = column // slab_rows * shard_rows + offset
    token = lax.broadcasted_iota(jnp.int32, score_shape, 0) // head_count
    visible = (offset < shard_rows) & ((place - token).astype(jnp.float32) < own_length + 1.0)
    whole = received.at[pl.ds(0, peer_count - 1)]
    pltpu.make_async_copy(whole, whole, recv_sem).wait()

    keys = received[...].reshape(peer_count * slab_rows, channels)
    scores = (
        lax.dot_general(
            query_rows, keys, (((1,), (1,)), ((), ())), preferred_element_type=jnp.float32
        )
        * score_scale
    )
    scores = jnp.where(visible, scores, floor_value)
    highest = jnp.max(scores, axis=1, keepdims=True)
    weights = jnp.where(visible, jnp.exp(scores - highest), 0.0)
    weight_sum = jnp.sum(weights, axis=1, keepdims=True)
    latent_total = jnp.dot(
        weights.astype(jnp.bfloat16), keys[:, :LATENT_WIDTH], preferred_element_type=jnp.float32
    )
    out_ref[...] = (latent_total / weight_sum).astype(jnp.bfloat16).reshape(out_ref.shape)
    pltpu.make_async_copy(whole, whole, send_sem).wait()


def padded_bytes(rows, columns):
    return rows * -(-columns // 128) * 128 * 4


def shards(cache, lengths, slots, query):
    wide_count = lax.axis_size("wide")
    narrow_count = lax.axis_size("narrow")
    peer_count = wide_count * narrow_count
    request_count, shard_rows, channels = cache.shape
    _, forward_steps, head_count, _ = query.shape
    slab_rows = pl.next_power_of_2(shard_rows)
    slabs = (request_count + peer_count) * slab_rows
    limit = (4 << 20) + 4 * padded_bytes(slabs, channels)
    return pl.pallas_call(
        functools.partial(kernel, wide_count, narrow_count),
        out_shape=jax.ShapeDtypeStruct((1, forward_steps, head_count, LATENT_WIDTH), jnp.bfloat16),
        in_specs=[pl.BlockSpec(memory_space=pltpu.HBM)] * 4,
        out_specs=pl.BlockSpec(memory_space=pltpu.VMEM),
        scratch_shapes=[
            pltpu.VMEM((shard_rows, request_count, channels), cache.dtype),
            pltpu.VMEM(lengths.shape, lengths.dtype),
            pltpu.VMEM(slots.shape, slots.dtype),
            pltpu.VMEM(query.shape, query.dtype),
            pltpu.VMEM((request_count, slab_rows, channels), cache.dtype),
            pltpu.VMEM((peer_count, slab_rows, channels), cache.dtype),
            pltpu.SemaphoreType.DMA((4,)),
            pltpu.SemaphoreType.DMA,
            pltpu.SemaphoreType.DMA,
        ],
        compiler_params=pltpu.CompilerParams(
            collective_id=0, has_side_effects=True, vmem_limit_bytes=limit
        ),
    )(*[
        pltpu.with_memory_space_constraint(argument, pltpu.HBM)
        for argument in (jnp.transpose(cache, (1, 0, 2)), lengths, slots, query)
    ])


def solution(mesh):
    return jax.shard_map(
        shards,
        mesh=mesh,
        in_specs=(
            P("grp", ("wide", "narrow"), None),
            P("grp"),
            P("grp"),
            P(("grp", "wide"), None, "narrow", None),
        ),
        out_specs=P(("grp", "wide"), None, "narrow", None),
        check_vma=False,
    )
```

profile of v0, /device:TPU:0, one launch (start us, length us, event | category | flops | bytes accessed | tf_op | source)
XLA Modules:
  0.0 9.6 jit_solution(209064092926078952)
XLA Ops:
  0.0 9.0 %shard_map.46 = bf16[1,1,32,512]{3,2,1,0:T(8,128)(2,1)S(1)} custom-call(bf16[3,8,576]{2,1,0:T(8,128)(2,1)} %bitcast.1, s32[8]{0:T(128)} %lengths_hbm.1, s32[8]{0:T(128)} %slots_hbm.1, bf16[1,1,32,576]{3,2,1,0:T(8,128)(2,1)} %query_hbm.1), custom_call_target="tpu_custom_call" | custom-call | tf_op jit(solution)/shard_map/pallas_call | solution.py:155
  9.0 0.6 %copy.6 = bf16[1,1,32,512]{3,2,1,0:T(8,128)(2,1)} copy(bf16[1,1,32,512]{3,2,1,0:T(8,128)(2,1)S(1)} %shard_map.46) | data formatting | bytes 65536
where the time goes:
time: 9.75 us; the launch traced here: 9.59 us
  Pallas kernels  8.96 us (92%)
  local copies, waits for them, and re-layouts  0.62 us (6%)
    pallas_call x1, Pallas kernels, shards(): pl.pallas_call(functools.partial(kernel, wide_count, narrow_count), out_s...  8.96 us
    unnamed x1, local copies, waits for them, and re-layouts  0.62 us

commit v1 on v0

v1 whole, which is shorter than its diff:
```python
import functools

import jax
import jax.numpy as jnp
from jax import lax
from jax.experimental import pallas as pl
from jax.experimental.pallas import tpu as pltpu
from jax.sharding import PartitionSpec as P

LATENT_WIDTH = 512
UNROLL_LIMIT = 16
GROUP_LIMIT = 4
DIRECT_LIMIT = 64

score_scale = 0.0721687836
floor_value = -1e30


def loop(count, body):
    if count <= UNROLL_LIMIT:
        for step in range(count):
            body(step)
    else:
        lax.fori_loop(0, count, lambda step, carry: (body(step), carry)[1], 0)


def kernel(
    wide_count,
    narrow_count,
    direct,
    cache_hbm,
    lengths_hbm,
    slots_hbm,
    query_hbm,
    out_ref,
    cache_ref,
    lengths_ref,
    slots_ref,
    query_ref,
    outgoing,
    received,
    direct_ref,
    local_sem,
    send_sem,
    recv_sem,
    direct_sem,
    arrived_sem,
):
    wide_index = lax.axis_index("wide")
    narrow_index = lax.axis_index("narrow")
    me = wide_index * narrow_count + narrow_index
    peer_count = wide_count * narrow_count
    shard_rows, request_count, channels = cache_ref.shape
    slab_rows = outgoing.shape[1]
    late_source = (wide_count - 1) * narrow_count

    cache_copy = pltpu.make_async_copy(cache_hbm, cache_ref, local_sem.at[1])
    slots_copy = pltpu.make_async_copy(slots_hbm, slots_ref, local_sem.at[0])
    lengths_copy = pltpu.make_async_copy(lengths_hbm, lengths_ref, local_sem.at[2])
    query_copy = pltpu.make_async_copy(query_hbm, query_ref, local_sem.at[3])
    cache_copy.start()
    slots_copy.start()

    def device(index):
        if isinstance(index, int):
            return {"wide": index // narrow_count, "narrow": index % narrow_count}
        return {"wide": lax.div(index, narrow_count), "narrow": lax.rem(index, narrow_count)}

    def signal(semaphore, index):
        pl.semaphore_signal(
            semaphore, inc=1, device_id=device(index), device_id_type=pl.DeviceIdType.MESH
        )

    hub = narrow_count - 1
    is_hub = me == hub
    group_wides = -(-(wide_count - 1) // GROUP_LIMIT)
    group_count = -(-(wide_count - 1) // group_wides)
    group = lax.div(wide_index + group_wides - 1, group_wides) - 1
    barrier = pltpu.get_barrier_semaphore()

    @pl.when((wide_index == 0) & ~is_hub)
    def _():
        signal(barrier, hub)

    pl.semaphore_wait(barrier, jnp.where(is_hub, narrow_count - 1, 1))

    if direct:
        direct_copy = pltpu.make_async_remote_copy(
            src_ref=cache_hbm,
            dst_ref=direct_ref,
            send_sem=direct_sem.at[0],
            recv_sem=direct_sem.at[1],
            device_id={"wide": 0, "narrow": 0},
            device_id_type=pl.DeviceIdType.MESH,
        )

        @pl.when(me == late_source)
        def _():
            direct_copy.start()

    @pl.when(wide_index > 0)
    def _():
        signal(arrived_sem.at[group], hub)

    def announce():
        loop(peer_count - narrow_count, lambda step: signal(barrier, peer_count - 1 - step))
        loop(narrow_count - 1, lambda step: signal(barrier, step))

    pl.when(is_hub)(announce)

    lengths_copy.start()
    query_copy.start()
    slots_copy.wait()
    slot_row = slots_ref[...].reshape(1, request_count)
    shape = (request_count * slab_rows, request_count)
    row = lax.broadcasted_iota(jnp.int32, shape, 0)
    picks = [
        (slot_row * slab_rows + offset == row).astype(jnp.float32).astype(jnp.bfloat16)
        for offset in range(shard_rows)
    ]
    cache_copy.wait()
    ordered = None
    for offset in range(shard_rows):
        term = jnp.dot(picks[offset], cache_ref[offset], preferred_element_type=jnp.float32)
        ordered = term if ordered is None else ordered + term
    outgoing[...] = ordered.reshape(outgoing.shape).astype(jnp.bfloat16)

    def send(index):
        target = device(index)
        wanted = index != me
        if direct and index == 0:
            wanted = wanted & (me != late_source)

        @pl.when(wanted)
        def _():
            pltpu.make_async_remote_copy(
                src_ref=outgoing.at[target["wide"]],
                dst_ref=received.at[me],
                send_sem=send_sem,
                recv_sem=recv_sem,
                device_id=target,
                device_id_type=pl.DeviceIdType.MESH,
            ).start()

    loop(narrow_count, send)
    received[me] = outgoing[wide_index]
    if direct:

        @pl.when(me == 0)
        def _():
            received[late_source] = jnp.zeros(received.shape[1:], received.dtype)

    for step in range(group_count):
        first = (1 + step * group_wides) * narrow_count
        last = min(1 + (step + 1) * group_wides, wide_count) * narrow_count

        @pl.when(is_hub)
        def _():
            pl.semaphore_wait(arrived_sem.at[step], last - first)
            announce()

        @pl.when(~is_hub)
        def _():
            pl.semaphore_wait(barrier, 1)

        loop(last - first, lambda at: send(at + first))

    lengths_copy.wait()
    query_copy.wait()
    own = slot_row == wide_index
    own_length = jnp.sum(
        jnp.where(own, lengths_ref[...].reshape(1, request_count).astype(jnp.float32), 0.0),
        axis=1,
        keepdims=True,
    )
    _, forward_steps, head_count, _ = query_ref.shape
    score_shape = (forward_steps * head_count, peer_count * slab_rows)
    query_rows = query_ref[...].reshape(score_shape[0], channels)
    column = lax.broadcasted_iota(jnp.int32, score_shape, 1)
    offset = column % slab_rows
    source = column // slab_rows
    place = source * shard_rows + offset
    token = lax.broadcasted_iota(jnp.int32, score_shape, 0) // head_count
    visible = (offset < shard_rows) & ((place - token).astype(jnp.float32) < own_length + 1.0)
    if direct:
        visible = visible & ((source != late_source) | (me != 0))
        square = (request_count, request_count)
        diagonal = lax.broadcasted_iota(jnp.int32, square, 0) == lax.broadcasted_iota(
            jnp.int32, square, 1
        )
        own_column = jnp.sum(jnp.where(diagonal & own, 1.0, 0.0), axis=1, keepdims=True)
        query_wide = query_rows.astype(jnp.float32)
        late_token = lax.broadcasted_iota(jnp.int32, (score_shape[0], 1), 0) // head_count
        late_visible = [
            (late_source * shard_rows + at - late_token).astype(jnp.float32) < own_length + 1.0
            for at in range(shard_rows)
        ]

    def wait_slabs(semaphore, spared):
        def wait(count):
            slabs = received.at[pl.ds(0, count)]
            pltpu.make_async_copy(slabs, slabs, semaphore).wait()

        if direct:
            pl.when(me == spared)(lambda: wait(peer_count - 2))
            pl.when(me != spared)(lambda: wait(peer_count - 1))
        else:
            wait(peer_count - 1)

    wait_slabs(recv_sem, 0)

    keys = received[...].reshape(peer_count * slab_rows, channels)
    scores = (
        lax.dot_general(
            query_rows, keys, (((1,), (1,)), ((), ())), preferred_element_type=jnp.float32
        )
        * score_scale
    )
    scores = jnp.where(visible, scores, floor_value)
    highest = jnp.max(scores, axis=1, keepdims=True)
    weights = jnp.where(visible, jnp.exp(scores - highest), 0.0)
    weight_sum = jnp.sum(weights, axis=1, keepdims=True)
    latent_total = jnp.dot(
        weights.astype(jnp.bfloat16), keys[:, :LATENT_WIDTH], preferred_element_type=jnp.float32
    )

    def finish(total, total_weight):
        out_ref[...] = (total / total_weight).astype(jnp.bfloat16).reshape(out_ref.shape)

    if direct:

        @pl.when(me != 0)
        def _():
            finish(latent_total, weight_sum)

        @pl.when(me == 0)
        def _():
            direct_copy.wait_recv()
            late_rows, late_scores, joint = [], [], highest
            for at in range(shard_rows):
                late_row = jnp.sum(
                    direct_ref[at].astype(jnp.float32) * own_column, axis=0, keepdims=True
                )
                score = jnp.sum(query_wide * late_row, axis=1, keepdims=True) * score_scale
                score = jnp.where(late_visible[at], score, floor_value)
                joint = jnp.maximum(joint, score)
                late_rows.append(late_row[:, :LATENT_WIDTH])
                late_scores.append(score)
            scale = jnp.exp(highest - joint)
            total_weight = weight_sum * scale
            total = latent_total * scale
            for at in range(shard_rows):
                weight = jnp.where(late_visible[at], jnp.exp(late_scores[at] - joint), 0.0)
                total_weight = total_weight + weight
                total = total + weight * late_rows[at]
            finish(total, total_weight)
    else:
        finish(latent_total, weight_sum)
    wait_slabs(send_sem, late_source)
    if direct:

        @pl.when(me == late_source)
        def _():
            direct_copy.wait_send()


def padded_bytes(rows, columns):
    return rows * -(-columns // 128) * 128 * 4


def shards(cache, lengths, slots, query):
    wide_count = lax.axis_size("wide")
    narrow_count = lax.axis_size("narrow")
    peer_count = wide_count * narrow_count
    request_count, shard_rows, channels = cache.shape
    _, forward_steps, head_count, _ = query.shape
    slab_rows = pl.next_power_of_2(shard_rows)
    direct = wide_count % 2 == 0 and request_count * shard_rows <= DIRECT_LIMIT
    group_wides = -(-(wide_count - 1) // GROUP_LIMIT)
    group_count = -(-(wide_count - 1) // group_wides)
    slabs = (request_count + peer_count) * slab_rows
    limit = (4 << 20) + 4 * padded_bytes(slabs, channels)
    return pl.pallas_call(
        functools.partial(kernel, wide_count, narrow_count, direct),
        out_shape=jax.ShapeDtypeStruct((1, forward_steps, head_count, LATENT_WIDTH), jnp.bfloat16),
        in_specs=[pl.BlockSpec(memory_space=pltpu.HBM)] * 4,
        out_specs=pl.BlockSpec(memory_space=pltpu.VMEM),
        scratch_shapes=[
            pltpu.VMEM((shard_rows, request_count, channels), cache.dtype),
            pltpu.VMEM(lengths.shape, lengths.dtype),
            pltpu.VMEM(slots.shape, slots.dtype),
            pltpu.VMEM(query.shape, query.dtype),
            pltpu.VMEM((request_count, slab_rows, channels), cache.dtype),
            pltpu.VMEM((peer_count, slab_rows, channels), cache.dtype),
            pltpu.VMEM((shard_rows, request_count, channels), cache.dtype),
            pltpu.SemaphoreType.DMA((4,)),
            pltpu.SemaphoreType.DMA,
            pltpu.SemaphoreType.DMA,
            pltpu.SemaphoreType.DMA((2,)),
            pltpu.SemaphoreType.REGULAR((group_count,)),
        ],
        compiler_params=pltpu.CompilerParams(
            collective_id=0, has_side_effects=True, vmem_limit_bytes=limit
        ),
    )(*[
        pltpu.with_memory_space_constraint(argument, pltpu.HBM)
        for argument in (jnp.transpose(cache, (1, 0, 2)), lengths, slots, query)
    ])


def solution(mesh):
    return jax.shard_map(
        shards,
        mesh=mesh,
        in_specs=(
            P("grp", ("wide", "narrow"), None),
            P("grp"),
            P("grp"),
            P(("grp", "wide"), None, "narrow", None),
        ),
        out_specs=P(("grp", "wide"), None, "narrow", None),
        check_vma=False,
    )
```

time: 9.75 us -> 9.2 us (0.944)
  Pallas kernels: 8.96 us -> 8.41 us
    pallas_call x1, Pallas kernels: 8.96 us -> 8.41 us  [shards(): pl.pallas_call(functools.partial(kernel, wide_count, narrow_count, direct...]
where the time goes in v1:
time: 9.2 us; the launch traced here: 9.03 us
  Pallas kernels  8.41 us (91%)
  local copies, waits for them, and re-layouts  0.62 us (7%)
    pallas_call x1, Pallas kernels, shards(): pl.pallas_call(functools.partial(kernel, wide_count, narrow_count, direct...  8.41 us
    unnamed x1, local copies, waits for them, and re-layouts  0.62 us

profile of v1, /device:TPU:0, one launch (start us, length us, event | category | flops | bytes accessed | tf_op | source)
XLA Modules:
  0.0 9.0 jit_solution(439332087573360305)
XLA Ops:
  0.0 8.4 %shard_map.46 = bf16[1,1,32,512]{3,2,1,0:T(8,128)(2,1)S(1)} custom-call(bf16[3,8,576]{2,1,0:T(8,128)(2,1)} %bitcast.1, s32[8]{0:T(128)} %lengths_hbm.1, s32[8]{0:T(128)} %slots_hbm.1, bf16[1,1,32,576]{3,2,1,0:T(8,128)(2,1)} %query_hbm.1), custom_call_target="tpu_custom_call" | custom-call | tf_op jit(solution)/shard_map/pallas_call | solution.py:283
  8.4 0.6 %copy.6 = bf16[1,1,32,512]{3,2,1,0:T(8,128)(2,1)} copy(bf16[1,1,32,512]{3,2,1,0:T(8,128)(2,1)S(1)} %shard_map.46) | data formatting | bytes 65536

commit v2 on v1

--- a/solution.py
+++ b/solution.py
@@ -40,10 +40,10 @@
     outgoing,
     received,
     direct_ref,
+    late_ref,
     local_sem,
-    send_sem,
     recv_sem,
-    direct_sem,
+    late_sem,
     arrived_sem,
 ):
     wide_index = lax.axis_index("wide")
@@ -54,10 +54,11 @@
     slab_rows = outgoing.shape[1]
     late_source = (wide_count - 1) * narrow_count
 
-    cache_copy = pltpu.make_async_copy(cache_hbm, cache_ref, local_sem.at[1])
-    slots_copy = pltpu.make_async_copy(slots_hbm, slots_ref, local_sem.at[0])
-    lengths_copy = pltpu.make_async_copy(lengths_hbm, lengths_ref, local_sem.at[2])
-    query_copy = pltpu.make_async_copy(query_hbm, query_ref, local_sem.at[3])
+    cache_copy = pltpu.make_async_copy(cache_hbm, cache_ref, local_sem.at[0])
+    send_sem = local_sem.at[0]
+    slots_copy = pltpu.make_async_copy(slots_hbm, slots_ref, local_sem.at[1])
+    query_copy = pltpu.make_async_copy(query_hbm, query_ref, local_sem.at[1])
+    lengths_copy = pltpu.make_async_copy(lengths_hbm, lengths_ref, local_sem.at[1])
     cache_copy.start()
     slots_copy.start()
 
@@ -88,13 +89,14 @@
         direct_copy = pltpu.make_async_remote_copy(
             src_ref=cache_hbm,
             dst_ref=direct_ref,
-            send_sem=direct_sem.at[0],
-            recv_sem=direct_sem.at[1],
-            device_id={"wide": 0, "narrow": 0},
+            send_sem=late_sem,
+            recv_sem=late_sem,
+            device_id=device(0),
             device_id_type=pl.DeviceIdType.MESH,
         )
-
-        @pl.when(me == late_source)
+        is_late_source = me == late_source
+
+        @pl.when(is_late_source)
         def _():
             direct_copy.start()
 
@@ -108,45 +110,50 @@
 
     pl.when(is_hub)(announce)
 
+    slots_copy.wait()
     lengths_copy.start()
-    query_copy.start()
-    slots_copy.wait()
     slot_row = slots_ref[...].reshape(1, request_count)
-    shape = (request_count * slab_rows, request_count)
+    shape = (request_count * slab_rows, shard_rows * request_count)
+    slot_tiled = jnp.concatenate([slot_row] * shard_rows, axis=1)
     row = lax.broadcasted_iota(jnp.int32, shape, 0)
-    picks = [
-        (slot_row * slab_rows + offset == row).astype(jnp.float32).astype(jnp.bfloat16)
-        for offset in range(shard_rows)
-    ]
+    column = lax.broadcasted_iota(jnp.int32, shape, 1)
+    pick = (slot_tiled * slab_rows + lax.div(column, request_count) == row).astype(jnp.float32)
+    pick = pick.astype(jnp.bfloat16)
     cache_copy.wait()
-    ordered = None
-    for offset in range(shard_rows):
-        term = jnp.dot(picks[offset], cache_ref[offset], preferred_element_type=jnp.float32)
-        ordered = term if ordered is None else ordered + term
-    outgoing[...] = ordered.reshape(outgoing.shape).astype(jnp.bfloat16)
-
-    def send(index):
+    shard = cache_ref[...].reshape(shard_rows * request_count, channels)
+    ordered = jnp.dot(pick, shard, preferred_element_type=jnp.float32)
+    outgoing[...] = ordered.astype(jnp.bfloat16).reshape(outgoing.shape)
+
+    def send(index, target_ref, target_sem, wanted):
         target = device(index)
-        wanted = index != me
-        if direct and index == 0:
-            wanted = wanted & (me != late_source)
 
         @pl.when(wanted)
         def _():
             pltpu.make_async_remote_copy(
                 src_ref=outgoing.at[target["wide"]],
-                dst_ref=received.at[me],
+                dst_ref=target_ref,
                 send_sem=send_sem,
-                recv_sem=recv_sem,
+                recv_sem=target_sem,
                 device_id=target,
                 device_id_type=pl.DeviceIdType.MESH,
             ).start()
 
-    loop(narrow_count, send)
+    def send_slab(index, wanted=True):
+        send(index, received.at[me], recv_sem, (index != me) & wanted)
+
+    for core in range(narrow_count):
+        if direct:
+            send_slab(core, ~is_late_source)
+            if core > 0:
+                send(core, late_ref, late_sem, is_late_source)
+        else:
+            send_slab(core)
+    lengths_copy.wait()
+    query_copy.start()
     received[me] = outgoing[wide_index]
     if direct:
 
-        @pl.when(me == 0)
+        @pl.when(wide_index == 0)
         def _():
             received[late_source] = jnp.zeros(received.shape[1:], received.dtype)
 
@@ -163,9 +170,8 @@
         def _():
             pl.semaphore_wait(barrier, 1)
 
-        loop(last - first, lambda at: send(at + first))
-
-    lengths_copy.wait()
+        loop(last - first, lambda at: send_slab(at + first))
+
     query_copy.wait()
     own = slot_row == wide_index
     own_length = jnp.sum(
@@ -183,31 +189,31 @@
     token = lax.broadcasted_iota(jnp.int32, score_shape, 0) // head_count
     visible = (offset < shard_rows) & ((place - token).astype(jnp.float32) < own_length + 1.0)
     if direct:
-        visible = visible & ((source != late_source) | (me != 0))
+        visible = visible & ((source != late_source) | (wide_index != 0))
         square = (request_count, request_count)
         diagonal = lax.broadcasted_iota(jnp.int32, square, 0) == lax.broadcasted_iota(
             jnp.int32, square, 1
         )
         own_column = jnp.sum(jnp.where(diagonal & own, 1.0, 0.0), axis=1, keepdims=True)
-        query_wide = query_rows.astype(jnp.float32)
+        query_wide = query_rows.astype(jnp.float32) * score_scale
         late_token = lax.broadcasted_iota(jnp.int32, (score_shape[0], 1), 0) // head_count
         late_visible = [
             (late_source * shard_rows + at - late_token).astype(jnp.float32) < own_length + 1.0
             for at in range(shard_rows)
         ]
 
-    def wait_slabs(semaphore, spared):
+    def wait_slabs(semaphore, one_fewer):
         def wait(count):
             slabs = received.at[pl.ds(0, count)]
             pltpu.make_async_copy(slabs, slabs, semaphore).wait()
 
         if direct:
-            pl.when(me == spared)(lambda: wait(peer_count - 2))
-            pl.when(me != spared)(lambda: wait(peer_count - 1))
+            pl.when(one_fewer)(lambda: wait(peer_count - 2))
+            pl.when(~one_fewer)(lambda: wait(peer_count - 1))
         else:
             wait(peer_count - 1)
 
-    wait_slabs(recv_sem, 0)
+    wait_slabs(recv_sem, wide_index == 0)
 
     keys = received[...].reshape(peer_count * slab_rows, channels)
     scores = (
@@ -229,22 +235,16 @@
 
     if direct:
 
-        @pl.when(me != 0)
+        @pl.when(wide_index != 0)
         def _():
             finish(latent_total, weight_sum)
 
-        @pl.when(me == 0)
-        def _():
-            direct_copy.wait_recv()
-            late_rows, late_scores, joint = [], [], highest
+        def fold(late_rows):
+            late_scores, joint = [], highest
             for at in range(shard_rows):
-                late_row = jnp.sum(
-                    direct_ref[at].astype(jnp.float32) * own_column, axis=0, keepdims=True
-                )
-                score = jnp.sum(query_wide * late_row, axis=1, keepdims=True) * score_scale
+                score = jnp.sum(query_wide * late_rows[at], axis=1, keepdims=True)
                 score = jnp.where(late_visible[at], score, floor_value)
                 joint = jnp.maximum(joint, score)
-                late_rows.append(late_row[:, :LATENT_WIDTH])
                 late_scores.append(score)
             scale = jnp.exp(highest - joint)
             total_weight = weight_sum * scale
@@ -252,14 +252,28 @@
             for at in range(shard_rows):
                 weight = jnp.where(late_visible[at], jnp.exp(late_scores[at] - joint), 0.0)
                 total_weight = total_weight + weight
-                total = total + weight * late_rows[at]
+                total = total + weight * late_rows[at][:, :LATENT_WIDTH]
             finish(total, total_weight)
+
+        @pl.when(me == 0)
+        def _():
+            direct_copy.wait_recv()
+            fold([
+                jnp.sum(direct_ref[at].astype(jnp.float32) * own_column, axis=0, keepdims=True)
+                for at in range(shard_rows)
+            ])
+
+        @pl.when((wide_index == 0) & (me != 0))
+        def _():
+            pltpu.make_async_copy(late_ref, late_ref, late_sem).wait()
+            late_slab = late_ref[...].astype(jnp.float32)
+            fold([late_slab[at : at + 1] for at in range(shard_rows)])
     else:
         finish(latent_total, weight_sum)
-    wait_slabs(send_sem, late_source)
-    if direct:
-
-        @pl.when(me == late_source)
+    wait_slabs(send_sem, is_late_source if direct else False)
+    if direct:
+
+        @pl.when(is_late_source)
         def _():
             direct_copy.wait_send()
 
@@ -293,10 +307,10 @@
             pltpu.VMEM((request_count, slab_rows, channels), cache.dtype),
             pltpu.VMEM((peer_count, slab_rows, channels), cache.dtype),
             pltpu.VMEM((shard_rows, request_count, channels), cache.dtype),
-            pltpu.SemaphoreType.DMA((4,)),
+            pltpu.VMEM((slab_rows, channels), cache.dtype),
+            pltpu.SemaphoreType.DMA((2,)),
             pltpu.SemaphoreType.DMA,
             pltpu.SemaphoreType.DMA,
-            pltpu.SemaphoreType.DMA((2,)),
             pltpu.SemaphoreType.REGULAR((group_count,)),
         ],
         compiler_params=pltpu.CompilerParams(

time: 9.2 us -> 9.15 us (level)
  no operation moved by 1% of the time
where the time goes in v2:
time: 9.15 us; the launch traced here: 8.97 us
  Pallas kernels  8.34 us (91%)
  local copies, waits for them, and re-layouts  0.62 us (7%)
    pallas_call x1, Pallas kernels, shards(): pl.pallas_call(functools.partial(kernel, wide_count, narrow_count, direct...  8.34 us
    unnamed x1, local copies, waits for them, and re-layouts  0.62 us

profile of v2, /device:TPU:0, one launch (start us, length us, event | category | flops | bytes accessed | tf_op | source)
XLA Modules:
  0.0 9.0 jit_solution(17485757145008684747)
XLA Ops:
  0.0 8.3 %shard_map.46 = bf16[1,1,32,512]{3,2,1,0:T(8,128)(2,1)S(1)} custom-call(bf16[3,8,576]{2,1,0:T(8,128)(2,1)} %bitcast.1, s32[8]{0:T(128)} %lengths_hbm.1, s32[8]{0:T(128)} %slots_hbm.1, bf16[1,1,32,576]{3,2,1,0:T(8,128)(2,1)} %query_hbm.1), custom_call_target="tpu_custom_call" | custom-call | tf_op jit(solution)/shard_map/pallas_call | solution.py:297
  8.4 0.6 %copy.6 = bf16[1,1,32,512]{3,2,1,0:T(8,128)(2,1)} copy(bf16[1,1,32,512]{3,2,1,0:T(8,128)(2,1)S(1)} %shard_map.46) | data formatting | bytes 65536

commit v3 on v2

--- a/solution.py
+++ b/solution.py
@@ -1,4 +1,5 @@
 import functools
+import math
 
 import jax
 import jax.numpy as jnp
@@ -59,8 +60,6 @@
     slots_copy = pltpu.make_async_copy(slots_hbm, slots_ref, local_sem.at[1])
     query_copy = pltpu.make_async_copy(query_hbm, query_ref, local_sem.at[1])
     lengths_copy = pltpu.make_async_copy(lengths_hbm, lengths_ref, local_sem.at[1])
-    cache_copy.start()
-    slots_copy.start()
 
     def device(index):
         if isinstance(index, int):
@@ -99,6 +98,9 @@
         @pl.when(is_late_source)
         def _():
             direct_copy.start()
+
+    cache_copy.start()
+    slots_copy.start()
 
     @pl.when(wide_index > 0)
     def _():
@@ -180,6 +182,7 @@
         keepdims=True,
     )
     _, forward_steps, head_count, _ = query_ref.shape
+    tile_heads = math.gcd(head_count, 8)
     score_shape = (forward_steps * head_count, peer_count * slab_rows)
     query_rows = query_ref[...].reshape(score_shape[0], channels)
     column = lax.broadcasted_iota(jnp.int32, score_shape, 1)
@@ -240,20 +243,25 @@
             finish(latent_total, weight_sum)
 
         def fold(late_rows):
-            late_scores, joint = [], highest
-            for at in range(shard_rows):
-                score = jnp.sum(query_wide * late_rows[at], axis=1, keepdims=True)
-                score = jnp.where(late_visible[at], score, floor_value)
-                joint = jnp.maximum(joint, score)
-                late_scores.append(score)
-            scale = jnp.exp(highest - joint)
-            total_weight = weight_sum * scale
-            total = latent_total * scale
-            for at in range(shard_rows):
-                weight = jnp.where(late_visible[at], jnp.exp(late_scores[at] - joint), 0.0)
-                total_weight = total_weight + weight
-                total = total + weight * late_rows[at][:, :LATENT_WIDTH]
-            finish(total, total_weight)
+            for token in range(forward_steps):
+                for head in range(0, head_count, tile_heads):
+                    rows = slice(token * head_count + head, token * head_count + head + tile_heads)
+                    late_scores, joint = [], highest[rows]
+                    for at in range(shard_rows):
+                        score = jnp.sum(query_wide[rows] * late_rows[at], axis=1, keepdims=True)
+                        score = jnp.where(late_visible[at][rows], score, floor_value)
+                        joint = jnp.maximum(joint, score)
+                        late_scores.append(score)
+                    scale = jnp.exp(highest[rows] - joint)
+                    total_weight = weight_sum[rows] * scale
+                    total = latent_total[rows] * scale
+                    for at in range(shard_rows):
+                        weight = jnp.exp(late_scores[at] - joint)
+                        weight = jnp.where(late_visible[at][rows], weight, 0.0)
+                        total_weight = total_weight + weight
+                        total = total + weight * late_rows[at][:, :LATENT_WIDTH]
+                    attended = (total / total_weight).astype(jnp.bfloat16)
+                    out_ref[0, token, head : head + tile_heads, :] = attended
 
         @pl.when(me == 0)
         def _():

time: 9.15 us -> 9.14 us (level)
  no operation moved by 1% of the time
where the time goes in v3:
time: 9.14 us; the launch traced here: 8.96 us
  Pallas kernels  8.34 us (91%)
  local copies, waits for them, and re-layouts  0.62 us (7%)
    pallas_call x1, Pallas kernels, shards(): pl.pallas_call(functools.partial(kernel, wide_count, narrow_count, direct...  8.34 us
    unnamed x1, local copies, waits for them, and re-layouts  0.62 us

profile of v3, /device:TPU:0, one launch (start us, length us, event | category | flops | bytes accessed | tf_op | source)
XLA Modules:
  0.0 9.0 jit_solution(2945973069137080352)
XLA Ops:
  0.0 8.3 %shard_map.46 = bf16[1,1,32,512]{3,2,1,0:T(8,128)(2,1)S(1)} custom-call(bf16[3,8,576]{2,1,0:T(8,128)(2,1)} %bitcast.1, s32[8]{0:T(128)} %lengths_hbm.1, s32[8]{0:T(128)} %slots_hbm.1, bf16[1,1,32,576]{3,2,1,0:T(8,128)(2,1)} %query_hbm.1), custom_call_target="tpu_custom_call" | custom-call | tf_op jit(solution)/shard_map/pallas_call | solution.py:305
  8.3 0.6 %copy.6 = bf16[1,1,32,512]{3,2,1,0:T(8,128)(2,1)} copy(bf16[1,1,32,512]{3,2,1,0:T(8,128)(2,1)S(1)} %shard_map.46) | data formatting | bytes 65536

commit v4 on v3

--- a/solution.py
+++ b/solution.py
@@ -13,7 +13,7 @@
 GROUP_LIMIT = 4
 DIRECT_LIMIT = 64
 
-score_scale = 0.0721687836
+score_scale = 0.0721687836 * math.log2(math.e)
 floor_value = -1e30
 
 
@@ -102,9 +102,13 @@
     cache_copy.start()
     slots_copy.start()
 
-    @pl.when(wide_index > 0)
+    @pl.when(group == 0)
     def _():
-        signal(arrived_sem.at[group], hub)
+        signal(barrier, hub)
+
+    @pl.when(group > 0)
+    def _():
+        signal(arrived_sem.at[group - 1], hub)
 
     def announce():
         loop(peer_count - narrow_count, lambda step: signal(barrier, peer_count - 1 - step))
@@ -165,7 +169,8 @@
 
         @pl.when(is_hub)
         def _():
-            pl.semaphore_wait(arrived_sem.at[step], last - first)
+            answered = barrier if step == 0 else arrived_sem.at[step - 1]
+            pl.semaphore_wait(answered, last - first)
             announce()
 
         @pl.when(~is_hub)
@@ -227,7 +232,7 @@
     )
     scores = jnp.where(visible, scores, floor_value)
     highest = jnp.max(scores, axis=1, keepdims=True)
-    weights = jnp.where(visible, jnp.exp(scores - highest), 0.0)
+    weights = jnp.exp2(scores - highest)
     weight_sum = jnp.sum(weights, axis=1, keepdims=True)
     latent_total = jnp.dot(
         weights.astype(jnp.bfloat16), keys[:, :LATENT_WIDTH], preferred_element_type=jnp.float32
@@ -252,12 +257,11 @@
                         score = jnp.where(late_visible[at][rows], score, floor_value)
                         joint = jnp.maximum(joint, score)
                         late_scores.append(score)
-                    scale = jnp.exp(highest[rows] - joint)
+                    scale = jnp.exp2(highest[rows] - joint)
                     total_weight = weight_sum[rows] * scale
                     total = latent_total[rows] * scale
                     for at in range(shard_rows):
-                        weight = jnp.exp(late_scores[at] - joint)
-                        weight = jnp.where(late_visible[at][rows], weight, 0.0)
+                        weight = jnp.exp2(late_scores[at] - joint)
                         total_weight = total_weight + weight
                         total = total + weight * late_rows[at][:, :LATENT_WIDTH]
                     attended = (total / total_weight).astype(jnp.bfloat16)
@@ -319,7 +323,7 @@
             pltpu.SemaphoreType.DMA((2,)),
             pltpu.SemaphoreType.DMA,
             pltpu.SemaphoreType.DMA,
-            pltpu.SemaphoreType.REGULAR((group_count,)),
+            pltpu.SemaphoreType.REGULAR((max(group_count - 1, 1),)),
         ],
         compiler_params=pltpu.CompilerParams(
             collective_id=0, has_side_effects=True, vmem_limit_bytes=limit

time: 9.14 us -> 9.13 us (level)
  no operation moved by 1% of the time
where the time goes in v4:
time: 9.13 us; the launch traced here: 8.95 us
  Pallas kernels  8.32 us (91%)
  local copies, waits for them, and re-layouts  0.62 us (7%)
    pallas_call x1, Pallas kernels, shards(): pl.pallas_call(functools.partial(kernel, wide_count, narrow_count, direct...  8.32 us
    unnamed x1, local copies, waits for them, and re-layouts  0.62 us

profile of v4, /device:TPU:0, one launch (start us, length us, event | category | flops | bytes accessed | tf_op | source)
XLA Modules:
  0.0 8.9 jit_solution(3114172859515753829)
XLA Ops:
  0.0 8.3 %shard_map.46 = bf16[1,1,32,512]{3,2,1,0:T(8,128)(2,1)S(1)} custom-call(bf16[3,8,576]{2,1,0:T(8,128)(2,1)} %bitcast.1, s32[8]{0:T(128)} %lengths_hbm.1, s32[8]{0:T(128)} %slots_hbm.1, bf16[1,1,32,576]{3,2,1,0:T(8,128)(2,1)} %query_hbm.1), custom_call_target="tpu_custom_call" | custom-call | tf_op jit(solution)/shard_map/pallas_call | solution.py:309
  8.3 0.6 %copy.6 = bf16[1,1,32,512]{3,2,1,0:T(8,128)(2,1)} copy(bf16[1,1,32,512]{3,2,1,0:T(8,128)(2,1)S(1)} %shard_map.46) | data formatting | bytes 65536

commit v5 on v4

--- a/solution.py
+++ b/solution.py
@@ -111,8 +111,8 @@
         signal(arrived_sem.at[group - 1], hub)
 
     def announce():
-        loop(peer_count - narrow_count, lambda step: signal(barrier, peer_count - 1 - step))
         loop(narrow_count - 1, lambda step: signal(barrier, step))
+        loop(peer_count - narrow_count, lambda step: signal(barrier, step + narrow_count))
 
     pl.when(is_hub)(announce)
 

time: 9.13 us -> 9.13 us (level)
  no operation moved by 1% of the time
where the time goes in v5:
time: 9.13 us; the launch traced here: 8.95 us
  Pallas kernels  8.32 us (91%)
  local copies, waits for them, and re-layouts  0.62 us (7%)
    pallas_call x1, Pallas kernels, shards(): pl.pallas_call(functools.partial(kernel, wide_count, narrow_count, direct...  8.32 us
    unnamed x1, local copies, waits for them, and re-layouts  0.62 us

profile of v5, /device:TPU:0, one launch (start us, length us, event | category | flops | bytes accessed | tf_op | source)
XLA Modules:
  0.0 8.9 jit_solution(7368364972822826628)
XLA Ops:
  0.0 8.3 %shard_map.46 = bf16[1,1,32,512]{3,2,1,0:T(8,128)(2,1)S(1)} custom-call(bf16[3,8,576]{2,1,0:T(8,128)(2,1)} %bitcast.1, s32[8]{0:T(128)} %lengths_hbm.1, s32[8]{0:T(128)} %slots_hbm.1, bf16[1,1,32,576]{3,2,1,0:T(8,128)(2,1)} %query_hbm.1), custom_call_target="tpu_custom_call" | custom-call | tf_op jit(solution)/shard_map/pallas_call | solution.py:309
  8.3 0.6 %copy.6 = bf16[1,1,32,512]{3,2,1,0:T(8,128)(2,1)} copy(bf16[1,1,32,512]{3,2,1,0:T(8,128)(2,1)S(1)} %shard_map.46) | data formatting | bytes 65536

commit v6 on v5

--- a/solution.py
+++ b/solution.py
@@ -177,7 +177,7 @@
         def _():
             pl.semaphore_wait(barrier, 1)
 
-        loop(last - first, lambda at: send_slab(at + first))
+        loop(last - first, lambda at: send_slab(last - 1 - at))
 
     query_copy.wait()
     own = slot_row == wide_index

time: 9.13 us -> 9.13 us (level)
  no operation moved by 1% of the time
where the time goes in v6:
time: 9.13 us; the launch traced here: 8.95 us
  Pallas kernels  8.32 us (91%)
  local copies, waits for them, and re-layouts  0.62 us (7%)
    pallas_call x1, Pallas kernels, shards(): pl.pallas_call(functools.partial(kernel, wide_count, narrow_count, direct...  8.32 us
    unnamed x1, local copies, waits for them, and re-layouts  0.62 us

profile of v6, /device:TPU:0, one launch (start us, length us, event | category | flops | bytes accessed | tf_op | source)
XLA Modules:
  0.0 8.9 jit_solution(8672287153327172782)
XLA Ops:
  0.0 8.3 %shard_map.46 = bf16[1,1,32,512]{3,2,1,0:T(8,128)(2,1)S(1)} custom-call(bf16[3,8,576]{2,1,0:T(8,128)(2,1)} %bitcast.1, s32[8]{0:T(128)} %lengths_hbm.1, s32[8]{0:T(128)} %slots_hbm.1, bf16[1,1,32,576]{3,2,1,0:T(8,128)(2,1)} %query_hbm.1), custom_call_target="tpu_custom_call" | custom-call | tf_op jit(solution)/shard_map/pallas_call | solution.py:309
  8.3 0.6 %copy.6 = bf16[1,1,32,512]{3,2,1,0:T(8,128)(2,1)} copy(bf16[1,1,32,512]{3,2,1,0:T(8,128)(2,1)S(1)} %shard_map.46) | data formatting | bytes 65536
